TPU v7x, 256 devices: a whole 4x4x8 slice. The times are simulated.
256 devices in a mesh: dp: 4 (over y_hi, core), seq: 64 (over z, x, y_lo).
Axes of the slice: x: 4, y: 4 (y_hi: 2, y_lo: 2; y = y_hi * 2 + y_lo), z: 8, core: 2. Of those that a mesh axis runs over, the one named last changes fastest.
Arguments:
- queries: bfloat16 [4, 8192, 2048], P('dp', 'seq'), may hold values from -12 to 12
- keys: bfloat16 [4, 8192, 512], P('dp', 'seq'), may hold values from -4 to 4
- values: bfloat16 [4, 8192, 512], P('dp', 'seq'), may hold values from -6 to 6
- segments: int32 [4, 8192], P('dp', 'seq'), may hold values from 0 to 3, never falling along the last dimension, each value on 1 to 7168 neighbouring positions
- task_ids: int32 [4], replicated, may hold values from 0 to 127
- prompt_keys: bfloat16 [128, 128, 512], P('seq'), may hold values from -4 to 4
- prompt_values: bfloat16 [128, 128, 512], P('seq'), may hold values from -6 to 6
- grad_out: bfloat16 [4, 8192, 2048], P('dp', 'seq'), may hold values from -6 to 6
Outputs:
- attended: bfloat16 [4, 8192, 2048], P('dp', 'seq')
- prompt_key_grad: float32 [128, 128, 512], P('seq')
- prompt_value_grad: float32 [128, 128, 512], P('seq')
Inputs may be any that keep to these rules, and one draw needn't show every extreme that they name: `segments`: along each example the document numbers never fall; one document holds 7168 tokens.
All inputs are finite; a program needn't handle non-finite values.
Results may differ from a plain program's by a relative error of at most 0.0096.
Values may be sent and summed in bfloat16 or wider, within the bound.
No kernel may reach another device: no remote copies, remote signals or barrier semaphores. Data moves between devices by JAX's collectives and lax.ppermute only.
A program may use at most 128 MiB of HBM per device.

v0:
```python
import math
import jax
import jax.numpy as jnp
from jax import lax
from jax.sharding import Mesh
from jax.sharding import PartitionSpec as P

KVH = 4
GROUP = 4
HD = 128
PROMPT = 128
SEQ = ("seq_0", "seq_1", "seq_2")
DP_SEQ = ("dp", "seq_0", "seq_1", "seq_2")


def laid_out(blocks, dim):
    blocks = jnp.moveaxis(blocks, 0, dim)
    lengths = blocks.shape
    return blocks.reshape(*lengths[:dim], lengths[dim] * lengths[dim + 1], *lengths[dim + 2 :])


def sent_to_all(shard, axis):
    devices = lax.axis_size(axis)
    return lax.all_to_all(
        jnp.broadcast_to(shard[None], (devices, *shard.shape)), axis, 0, 0, tiled=True
    )


def gather_directly(shard, axis, dim):
    return laid_out(sent_to_all(shard, axis), dim)


def broadcast_by_axis(shard, axes, root):
    shard = jnp.where(lax.axis_index(axes) == root, shard, jnp.zeros_like(shard))
    for axis in axes:
        shard = lax.psum(shard, axis)
    return shard


def piece_ends(length, count):
    unit = 8 if length >= 8 * count else 1
    return [length // unit * k // count * unit for k in range(1, count)]


def gather_in_order(shard, axes, turns):
    blocks = shard
    for k in turns:
        blocks = lax.all_gather(blocks, axes[k])
    done = turns[::-1]
    back = [done.index(k) for k in range(len(axes))]
    blocks = blocks.transpose(*back, *range(len(axes), blocks.ndim))
    return blocks.reshape(-1, *shard.shape)


def gather_all_axes(shard, axes, dim):
    cut = max(range(max(1, shard.ndim - 1)), key=lambda d: shard.shape[d])
    count, gathered = (len(axes), [])
    for initial, piece in enumerate(
        jnp.split(shard, piece_ends(shard.shape[cut], count), axis=cut)
    ):
        if piece.size:
            turns = [(initial - k) % count for k in range(count)]
            gathered.append(gather_in_order(piece, axes, turns))
    return laid_out(jnp.concatenate(gathered, axis=cut + 1), dim)


def shards(queries, keys, values, segments, task_ids, prompt_keys, prompt_values, grad_out):
    tok_rows = queries.shape[1]
    scaling = 1.0 / math.sqrt(HD)
    seq_rank = lax.axis_index(SEQ)
    query_heads = queries[0].reshape(tok_rows, KVH, GROUP, HD)
    query_segments = segments[0]
    query_index = seq_rank * tok_rows + lax.iota(jnp.int32, tok_rows)
    all_segments = gather_directly(segments[0], SEQ, 0)
    bank_size = prompt_keys.shape[0]
    my_task = task_ids[lax.axis_index("dp")]
    prompt_owner = my_task // bank_size
    bank_slot = my_task % bank_size
    local_pair = jnp.stack(
        [
            lax.dynamic_index_in_dim(prompt_keys, bank_slot, 0, keepdims=False),
            lax.dynamic_index_in_dim(prompt_values, bank_slot, 0, keepdims=False),
        ]
    )
    shared_pair = broadcast_by_axis(local_pair, SEQ, prompt_owner)
    prompt_key_heads = shared_pair[0].reshape(PROMPT, KVH, HD)
    prompt_value_heads = shared_pair[1].reshape(PROMPT, KVH, HD)
    prompt_scores = (
        jnp.einsum(
            "tkgd,pkd->tkgp", query_heads, prompt_key_heads, preferred_element_type=jnp.float32
        )
        * scaling
    )
    maximum = jnp.max(prompt_scores, axis=-1)
    weights = jnp.exp(prompt_scores - maximum[..., None])
    totals = jnp.sum(weights, axis=-1)
    accumulated = jnp.einsum(
        "tkgp,pkd->tkgd",
        weights.astype(jnp.bfloat16),
        prompt_value_heads,
        preferred_element_type=jnp.float32,
    )
    carried = (maximum, totals, accumulated)

    def absorb_rows(state_now, stacked, first_row):
        key_count = stacked.shape[1]
        key_index = first_row + lax.iota(jnp.int32, key_count)
        key_segments = lax.dynamic_slice_in_dim(
            all_segments, jnp.maximum(first_row, 0), key_count, 0
        )
        key_mask = (
            (key_segments[None, :] == query_segments[:, None])
            & (key_index[None, :] <= query_index[:, None])
            & True
        )

        def update(inner_state):
            old_peak, old_totals, old_accum = inner_state
            key_heads = stacked[0].reshape(key_count, KVH, HD)
            value_heads = stacked[1].reshape(key_count, KVH, HD)
            scores = (
                jnp.einsum(
                    "tkgd,skd->tkgs", query_heads, key_heads, preferred_element_type=jnp.float32
                )
                * scaling
            )
            mask_wide = key_mask[:, None, None, :]
            new_peak = jnp.maximum(
                old_peak, jnp.max(jnp.where(mask_wide, scores, -jnp.inf), axis=-1)
            )
            shrink = jnp.exp(old_peak - new_peak)
            block_weights = jnp.where(mask_wide, jnp.exp(scores - new_peak[..., None]), 0.0)
            new_totals = old_totals * shrink + jnp.sum(block_weights, axis=-1)
            new_accum = old_accum * shrink[..., None] + jnp.einsum(
                "tkgs,skd->tkgd",
                block_weights.astype(jnp.bfloat16),
                value_heads,
                preferred_element_type=jnp.float32,
            )
            return (new_peak, new_totals, new_accum)

        return lax.cond(jnp.any(key_mask), update, lambda inner_state: inner_state, state_now)

    own_pair = jnp.stack([keys[0], values[0]])
    stacked = gather_all_axes(own_pair, SEQ, 1)
    key_count = stacked.shape[1]
    tile_rows = 512

    def loop_tile(block_index, inner_state):
        offset = block_index * tile_rows
        piece = lax.dynamic_slice_in_dim(stacked, offset, tile_rows, 1)
        return absorb_rows(inner_state, piece, offset)

    carried = lax.fori_loop(0, key_count // tile_rows, loop_tile, carried)
    maximum, totals, accumulated = carried
    attended = (accumulated / totals[..., None]).astype(jnp.bfloat16)
    log_norm = maximum + jnp.log(totals)
    grad_heads = grad_out[0].reshape(tok_rows, KVH, GROUP, HD)
    attended_wide = lax.optimization_barrier(attended).astype(jnp.float32)
    row_delta = jnp.sum(grad_heads.astype(jnp.float32) * attended_wide, axis=-1)
    prompt_probs = jnp.exp(prompt_scores - log_norm[..., None])
    prompt_dots = jnp.einsum(
        "tkgd,pkd->tkgp", grad_heads, prompt_value_heads, preferred_element_type=jnp.float32
    )
    score_grad = prompt_probs * (prompt_dots - row_delta[..., None])
    value_part = jnp.einsum(
        "tkgp,tkgd->pkd",
        prompt_probs.astype(jnp.bfloat16),
        grad_heads,
        preferred_element_type=jnp.float32,
    )
    key_part = (
        jnp.einsum(
            "tkgp,tkgd->pkd",
            score_grad.astype(jnp.bfloat16),
            query_heads,
            preferred_element_type=jnp.float32,
        )
        * scaling
    )
    value_part = value_part.reshape(PROMPT, KVH * HD)
    key_part = key_part.reshape(PROMPT, KVH * HD)
    group_size = lax.axis_size("dp")
    group_rank = lax.axis_index("dp")
    slot_match = (lax.iota(jnp.int32, group_size) == group_rank)[:, None, None]
    key_buffer = jnp.where(slot_match, key_part[None], 0.0)
    value_buffer = jnp.where(slot_match, value_part[None], 0.0)
    key_all, value_all = lax.psum((key_buffer, value_buffer), DP_SEQ)
    own_tasks = seq_rank * bank_size + lax.iota(jnp.int32, bank_size)
    matches = (task_ids[:, None] == own_tasks[None, :])[:, :, None, None]
    key_grad = jnp.sum(jnp.where(matches, key_all[:, None], 0.0), axis=0)
    value_grad = jnp.sum(jnp.where(matches, value_all[:, None], 0.0), axis=0)
    return (attended.reshape(1, tok_rows, KVH * GROUP * HD), key_grad, value_grad)


def solution(mesh):
    split = Mesh(mesh.devices.reshape(mesh.shape["dp"], 8, 4, 2), ("dp", "seq_0", "seq_1", "seq_2"))
    return jax.shard_map(
        shards,
        mesh=split,
        in_specs=(
            P("dp", SEQ, None),
            P("dp", SEQ, None),
            P("dp", SEQ, None),
            P("dp", SEQ),
            P(),
            P(SEQ, None, None),
            P(SEQ, None, None),
            P("dp", SEQ, None),
        ),
        out_specs=(P("dp", SEQ, None), P(SEQ, None, None), P(SEQ, None, None)),
        check_vma=False,
    )
```

profile of v0, /device:TPU:2, one launch (start us, length us, event | category | flops | bytes accessed | tf_op | source)
XLA Modules:
  0.0 886.4 jit_solution(14403823708301323526)
XLA Ops:
  8.0 1.2 dynamic_slice.28
  11.9 1.0 constant_dynamic-slice_fusion.2
  14.0 0.9 constant_dynamic-update-slice_fusion.1
  14.9 0.9 constant_dynamic-update-slice_fusion
  15.8 74.2 %all-reduce.6.cloned.1.call-done = bf16[2,128,512]{1,2,0:T(8,128)(2,1)} async-done(((bf16[2,128,512]{1,2,0:T(8,128)(2,1)}), bf16[2,128,512]{1,2,0:T(8,128)(2,1)}) %all-reduce.6.cloned.1.call-update) | async-done | bytes 262160 | tf_op jit(solution)/shard_map/psum | solution.py:36
  90.2 27.7 %all-gather = bf16[16,40,512]{2,1,0:T(8,128)(2,1)} all-gather(bf16[2,40,512]{2,1,0:T(8,128)(2,1)S(1)} %get-tuple-element.363), channel_id=2, replica_groups=mesh['dp'=4,'seq_0'=8,'seq_1'=4,'seq_2'=2] {'seq_0'}, dimensions={0}, use_global_device_ids=true | all-gather | bytes 737280 | tf_op jit(solution)/shard_map/all_gather | solution.py:48
  117.9 13.2 %all-gather.3 = bf16[8,40,512]{2,1,0:T(8,128)(2,1)} all-gather(bf16[2,40,512]{2,1,0:T(8,128)(2,1)S(1)} %get-tuple-element.364), channel_id=5, replica_groups=mesh['dp'=4,'seq_0'=8,'seq_1'=4,'seq_2'=2] {'seq_1'}, dimensions={0}, use_global_device_ids=true | all-gather | bytes 409600 | tf_op jit(solution)/shard_map/all_gather | solution.py:48
  131.2 5.5 all-reduce.8.cloned.1.call-done
  136.7 9.0 %all-gather.15.cloned.1.call-done = bf16[16,2,40,512]{3,2,1,0:T(8,128)(2,1)} async-done(((bf16[8,2,40,512]{3,2,1,0:T(8,128)(2,1)}), bf16[16,2,40,512]{3,2,1,0:T(8,128)(2,1)}) %all-gather.15.cloned.1.call-update) | async-done | bytes 1310736 | tf_op jit(solution)/shard_map/all_gather | solution.py:48
  145.8 44.8 %all-gather.19.cloned.1.call-done = bf16[32,2,40,512]{3,2,1,0:T(8,128)(2,1)} async-done(((bf16[4,2,40,512]{3,2,1,0:T(8,128)(2,1)}), bf16[32,2,40,512]{3,2,1,0:T(8,128)(2,1)}) %all-gather.19.cloned.1.call-update) | async-done | bytes 2621456 | tf_op jit(solution)/shard_map/all_gather | solution.py:48
  190.7 5.3 all-gather.6
  196.0 14.8 %all-gather.7 = bf16[8,2,48,512]{3,2,1,0:T(8,128)(2,1)} all-gather(bf16[2,2,48,512]{3,2,1,0:T(8,128)(2,1)S(1)} %bitcast.153), channel_id=9, replica_groups=mesh['dp'=4,'seq_0'=8,'seq_1'=4,'seq_2'=2] {'seq_1'}, dimensions={0}, use_global_device_ids=true | all-gather | bytes 983040 | tf_op jit(solution)/shard_map/all_gather | solution.py:48
  211.5 8.6 all-to-all-start
  221.0 5.4 all-reduce.10.cloned.1.call-done
  226.4 1.0 fusion.40
  227.7 1.3 convolution_bitcast_fusion.1
  229.0 2.6 copy.151
  231.8 56.3 %all-gather.17.cloned.1.call-done = bf16[8,8,2,40,512]{4,3,2,1,0:T(8,128)(2,1)} async-done(((bf16[2,8,2,40,512]{4,3,2,1,0:T(8,128)(2,1)}), bf16[8,8,2,40,512]{4,3,2,1,0:T(8,128)(2,1)}) %all-gather.17.cloned.1.call-update) | async-done | bytes 5242896 | tf_op jit(solution)/shard_map/all_gather | solution.py:48
  288.1 5.3 copy.148
  293.4 71.0 %all-gather.21.cloned.1.call-done = bf16[16,4,2,40,512]{4,3,2,1,0:T(8,128)(2,1)} async-done(((bf16[8,4,2,40,512]{4,3,2,1,0:T(8,128)(2,1)}), bf16[16,4,2,40,512]{4,3,2,1,0:T(8,128)(2,1)}) %all-gather.21.cloned.1.call-update) | async-done | bytes 5242896 | tf_op jit(solution)/shard_map/all_gather | solution.py:48
  364.4 5.3 copy.149
  369.7 72.0 %all-gather.23.cloned.1.call-done = bf16[32,2,2,48,512]{4,3,2,1,0:T(8,128)(2,1)} async-done(((bf16[4,2,2,48,512]{4,3,2,1,0:T(8,128)(2,1)}), bf16[32,2,2,48,512]{4,3,2,1,0:T(8,128)(2,1)}) %all-gather.23.cloned.1.call-update) | async-done | bytes 6291472 | tf_op jit(solution)/shard_map/all_gather | solution.py:48
  441.6 13.6 %maximum_bitcast_fusion = bf16[2,64,128,512]{3,2,0,1:T(8,128)(2,1)} fusion(bf16[64,2,48,512]{3,2,1,0:T(8,128)(2,1)} %bitcast.137, bf16[64,2,40,512]{3,2,1,0:T(8,128)(2,1)} %bitcast.129, bf16[64,2,40,512]{3,2,1,0:T(8,128)(2,1)} %bitcast.128), kind=kLoop, calls=%fused_computation.24 | loop fusion | flops 50331648 | bytes 33554432 | tf_op jit(solution)/shard_map/transpose | solution.py:17
  455.3 23.1 %copy.150 = bf16[2,64,128,512]{2,1,3,0:T(8,128)(2,1)} copy(bf16[2,64,128,512]{3,2,0,1:T(8,128)(2,1)} %maximum_bitcast_fusion) | data formatting | bytes 33554432 | tf_op jit(solution)/shard_map/transpose | solution.py:17
  478.4 25.3 %reshape.89 = bf16[2,8192,512]{1,2,0:T(8,128)(2,1)} reshape(bf16[2,64,128,512]{2,1,3,0:T(8,128)(2,1)} %copy.150) | data formatting | bytes 33554432 | tf_op jit(solution)/shard_map/reshape | solution.py:19
  503.7 32.3 %while.18 = (s32[]{:T(128)}, f32[128,4,4]{0,2,1:T(4,128)S(1)}, f32[128,4,4]{0,2,1:T(4,128)S(1)}, f32[128,4,4,128]{3,0,2,1:T(8,128)}, s32[8192]{0:T(1024)S(1)}, /...) while((s32[]{:T(128)}, f32[128,4,4]{0,2,1:T(4,128)S(1)}, ...), condition=%wide.region_11.12_spmd.clone, body=%wide.region_5.11_spmd.clone.sunk | while | flops 549196416 | bytes 27144060 | solution.py:154
  503.8 0.9 fusion.53
  505.4 5.6 conditional.3
  505.4 1.3 constant_dynamic-slice_fusion.1
  508.4 1.5 fusion.16
  510.0 1.0 copy-done.1
  512.7 0.9 fusion.53
  514.4 0.9 fusion.53
  516.0 0.9 fusion.53
  517.7 0.9 fusion.53
  519.4 0.9 fusion.53
  521.1 0.9 fusion.53
  524.4 0.9 fusion.53
  526.1 0.9 fusion.53
  527.8 0.9 fusion.53
  531.1 0.9 fusion.53
  532.8 0.9 fusion.53
  536.0 2.5 copy.153
  538.5 1.3 divide_convert_fusion
  541.2 1.7 broadcast_select_fusion.1
  543.0 1.0 copy.161
  544.0 332.2 %all-reduce.12.cloned.1.call-done = (f32[4,128,512]{2,1,0:T(8,128)}, f32[4,128,512]{2,1,0:T(8,128)}) async-done(((f32[4,128,512]{2,1,0:T(8,128)}, f32[4,128,512]{2,1,0:T(8,128)}), (f32[4,128,512]{2,1,0:T(8,128)}, f32[4,128,512]{2,1,0:T(8,128)})) %all-reduce.12.cloned.1.call-update) | async-done | bytes 2097168 | tf_op jit(solution)/shard_map/psum | solution.py:188
  876.3 3.0 select_reduce_fusion
  (122 shorter events, 11.9 us)
Async XLA Ops:
  8.0 82.1 %all-reduce.6.cloned.1.call-start = ((), (), s32[]{:S(2)}) async-start(), calls=%async_computation.1 | async-start | bytes 524288 | tf_op jit(solution)/shard_map/psum | solution.py:36
  13.9 122.7 %all-reduce.8.cloned.1.call-start = ((), (), s32[]{:S(2)}) async-start(), calls=%async_computation.2 | async-start | bytes 524288 | tf_op jit(solution)/shard_map/psum | solution.py:36
  90.1 55.7 %all-gather.15.cloned.1.call-start = ((), (), s32[]{:S(2)}) async-start(), calls=%async_computation.4 | async-start | bytes 1966080 | tf_op jit(solution)/shard_map/all_gather | solution.py:48
  90.1 120.7 %copy-start.4 = (s32[1,128]{1,0:T(1,128)S(1)}, s32[1,128]{1,0:T(1,128)}, u32[]{:S(2)}) copy-start(s32[1,128]{1,0:T(1,128)} %param.15) | copy-start | bytes 1540
  90.1 130.0 %copy-start.2 = (bf16[1,128,2048]{2,1,0:T(8,128)(2,1)S(1)}, bf16[1,128,2048]{2,1,0:T(8,128)(2,1)}, u32[]{:S(2)}) copy-start(bf16[1,128,2048]{2,1,0:T(8,128)(2,1)} %param.12) | copy-start | bytes 1572868
  117.8 72.8 %all-gather.19.cloned.1.call-start = ((), (), s32[]{:S(2)}) async-start(), calls=%async_computation.6 | async-start | bytes 2949120 | tf_op jit(solution)/shard_map/all_gather | solution.py:48
  131.1 95.2 %all-reduce.10.cloned.1.call-start = ((), (), s32[]{:S(2)}) async-start(), calls=%async_computation.3 | async-start | bytes 524288 | tf_op jit(solution)/shard_map/psum | solution.py:36
  136.7 151.4 %all-gather.17.cloned.1.call-start = ((), (), s32[]{:S(2)}) async-start(), calls=%async_computation.5 | async-start | bytes 6553600 | tf_op jit(solution)/shard_map/all_gather | solution.py:48
  145.8 75.0 %copy-start.3 = (bf16[1,128,2048]{2,1,0:T(8,128)(2,1)S(1)}, bf16[1,128,2048]{2,1,0:T(8,128)(2,1)}, u32[]{:S(2)}) copy-start(bf16[1,128,2048]{2,1,0:T(8,128)(2,1)} %param.19) | copy-start | bytes 1572868
  145.8 218.6 %all-gather.21.cloned.1.call-start = ((), (), s32[]{:S(2)}) async-start(), calls=%async_computation.7 | async-start | bytes 7864320 | tf_op jit(solution)/shard_map/all_gather | solution.py:48
  190.6 251.0 %all-gather.23.cloned.1.call-start = ((), (), s32[]{:S(2)}) async-start(), calls=%async_computation.8 | async-start | bytes 7077888 | tf_op jit(solution)/shard_map/all_gather | solution.py:48
  211.5 292.2 %all-to-all-start = ((s32[64,1,128]{2,1,0:T(1,128)}), s32[64,1,128]{2,1,0:T(1,128)S(1)}, u32[]{:S(2)}, u32[]{:S(2)}) async-start(s32[64,1,128]{2,1,0:T(1,128)} %broadcast_in_dim.114), calls=%async_computation | async-start | bytes 65536 | tf_op jit(solution)/shard_map/all_to_all | solution.py:24
  220.1 656.2 %all-reduce.12.cloned.1.call-start = ((), (), s32[]{:S(2)}) async-start(), calls=%async_computation.9 | async-start | bytes 4194304 | tf_op jit(solution)/shard_map/psum | solution.py:188
  506.7 1.8 copy-start
  510.0 1.0 copy-start.1
  540.4 2.5 copy-start.5
Sparse Core Ops, SparseCore 0:
  14.1 75.9 all-reduce.5
  92.4 44.2 all-reduce.7
  543.1 333.1 all-reduce.11
Sparse Core Ops, SparseCore 1:
  117.9 27.8 all-gather.14
  147.4 43.1 all-gather.18
  193.1 33.3 all-reduce.9
  228.2 59.8 all-gather.16
  289.9 74.5 all-gather.20
  366.2 75.4 all-gather.22
where the time goes:
time: 889 us; the launch traced here: 886 us
  waiting for transfers between devices  670 us (75%)
  local copies, waits for them, and re-layouts  75.8 us (9%)
  blocking collectives  61 us (7%)
  other arithmetic  36.2 us (4%)
  between operations  18.1 us (2%)
  loops' own time  10.9 us (1%)
  starting transfers between devices  8.97 us (1%)
    psum x1, waiting for transfers between devices, shards(): key_all, value_all = lax.psum((key_buffer, value_buffer), DP_SEQ)  332 us
    all_gather x5, waiting for transfers between devices, gather_in_order(): blocks = lax.all_gather(blocks, axes[k])  253 us
    psum x3, waiting for transfers between devices, broadcast_by_axis(): shard = lax.psum(shard, axis)  85 us
    all_gather x4, blocking collectives, gather_in_order(): blocks = lax.all_gather(blocks, axes[k])  61 us
    reshape x1, local copies, waits for them, and re-layouts, laid_out(): blocks.reshape(*lengths[:dim], lengths[dim] * lengths[dim + 1], *lengths[...  25.3 us
    transpose x1, local copies, waits for them, and re-layouts, laid_out(): blocks = jnp.moveaxis(blocks, 0, dim)  23.1 us
  transfers between devices with their start and end apart: 10, of which 9 were waited for; matrix products, arithmetic and copies ran while one was open for 9% of the time, Pallas kernels for 0%

commit v1 on v0

--- a/solution.py
+++ b/solution.py
@@ -33,7 +33,7 @@
 def broadcast_by_axis(shard, axes, root):
     shard = jnp.where(lax.axis_index(axes) == root, shard, jnp.zeros_like(shard))
     for axis in axes:
-        shard = lax.psum(shard, axis)
+        shard = lax.all_gather(shard, axis).sum(axis=0)
     return shard
 
 

time: 889 us -> 822 us (0.925)
  waiting for transfers between devices: 670 us -> 589 us
  blocking collectives: 61 us -> 74 us
    psum x3 -> x0, waiting for transfers between devices: 85 us -> none  [broadcast_by_axis(): shard = lax.psum(shard, axis)]
  transfers between devices with their start and end apart: 10 -> 9, of which waited for: 9 -> 6; matrix products, arithmetic and copies ran while one was open for 9% -> 11% of each run, Pallas kernels for 0% -> 0%
where the time goes in v1:
time: 822 us; the launch traced here: 819 us
  waiting for transfers between devices  589 us (72%)
  local copies, waits for them, and re-layouts  75 us (9%)
  blocking collectives  74 us (9%)
  other arithmetic  39.5 us (5%)
  between operations  17 us (2%)
  loops' own time  11.3 us (1%)
  starting transfers between devices  8.83 us (1%)
    psum x1, waiting for transfers between devices, shards(): key_all, value_all = lax.psum((key_buffer, value_buffer), DP_SEQ)  333 us
    all_gather x5, waiting for transfers between devices, gather_in_order(): blocks = lax.all_gather(blocks, axes[k])  256 us
    all_gather x4, blocking collectives, gather_in_order(): blocks = lax.all_gather(blocks, axes[k])  66.7 us
    reshape x1, local copies, waits for them, and re-layouts, laid_out(): blocks.reshape(*lengths[:dim], lengths[dim] * lengths[dim + 1], *lengths[...  25.3 us
    transpose x1, local copies, waits for them, and re-layouts, laid_out(): blocks = jnp.moveaxis(blocks, 0, dim)  23.2 us
  transfers between devices with their start and end apart: 9, of which 6 were waited for; matrix products, arithmetic and copies ran while one was open for 11% of the time, Pallas kernels for 0%

profile of v1, /device:TPU:2, one launch (start us, length us, event | category | flops | bytes accessed | tf_op | source)
XLA Modules:
  0.0 819.4 jit_solution(6419911136234508713)
XLA Ops:
  7.2 1.2 dynamic_slice.28
  11.1 1.0 dynamic-slice_bitcast_fusion
  12.9 0.9 constant_dynamic-update-slice_fusion.1
  13.8 0.9 constant_dynamic-update-slice_fusion
  14.8 32.7 %all-gather.2 = bf16[16,40,512]{2,1,0:T(8,128)(2,1)} all-gather(bf16[2,40,512]{2,1,0:T(8,128)(2,1)S(1)} %get-tuple-element.363), channel_id=4, replica_groups=mesh['dp'=4,'seq_0'=8,'seq_1'=4,'seq_2'=2] {'seq_0'}, dimensions={0}, use_global_device_ids=true | all-gather | bytes 737280 | tf_op jit(solution)/shard_map/all_gather | solution.py:48
  47.5 13.0 %all-gather.5 = bf16[8,40,512]{2,1,0:T(8,128)(2,1)} all-gather(bf16[2,40,512]{2,1,0:T(8,128)(2,1)S(1)} %get-tuple-element.364), channel_id=7, replica_groups=mesh['dp'=4,'seq_0'=8,'seq_1'=4,'seq_2'=2] {'seq_1'}, dimensions={0}, use_global_device_ids=true | all-gather | bytes 409600 | tf_op jit(solution)/shard_map/all_gather | solution.py:48
  60.7 2.7 reduce_sum.82
  63.4 24.4 %all-gather.23.cloned.1.call-done = bf16[16,2,40,512]{3,2,1,0:T(8,128)(2,1)} async-done(((bf16[8,2,40,512]{3,2,1,0:T(8,128)(2,1)}), bf16[16,2,40,512]{3,2,1,0:T(8,128)(2,1)}) %all-gather.23.cloned.1.call-update) | async-done | bytes 1310736 | tf_op jit(solution)/shard_map/all_gather | solution.py:48
  87.9 44.9 %all-gather.27.cloned.1.call-done = bf16[32,2,40,512]{3,2,1,0:T(8,128)(2,1)} async-done(((bf16[4,2,40,512]{3,2,1,0:T(8,128)(2,1)}), bf16[32,2,40,512]{3,2,1,0:T(8,128)(2,1)}) %all-gather.27.cloned.1.call-update) | async-done | bytes 2621456 | tf_op jit(solution)/shard_map/all_gather | solution.py:48
  132.8 5.3 all-gather.8
  138.1 15.7 %all-gather.9 = bf16[8,2,48,512]{3,2,1,0:T(8,128)(2,1)} all-gather(bf16[2,2,48,512]{3,2,1,0:T(8,128)(2,1)S(1)} %bitcast.161), channel_id=11, replica_groups=mesh['dp'=4,'seq_0'=8,'seq_1'=4,'seq_2'=2] {'seq_1'}, dimensions={0}, use_global_device_ids=true | all-gather | bytes 983040 | tf_op jit(solution)/shard_map/all_gather | solution.py:48
  154.5 8.5 %all-to-all-start = ((s32[64,1,128]{2,1,0:T(1,128)}), s32[64,1,128]{2,1,0:T(1,128)S(1)}, u32[]{:S(2)}, u32[]{:S(2)}) async-start(s32[64,1,128]{2,1,0:T(1,128)} %broadcast_in_dim.114), calls=%async_computation | async-start | bytes 65536 | tf_op jit(solution)/shard_map/all_to_all | solution.py:24
  164.0 1.5 reduce_sum.83
  165.5 7.3 all-gather.1
  173.5 1.3 convolution_bitcast_fusion.1
  174.8 2.7 copy.142
  177.7 44.0 %all-gather.25.cloned.1.call-done = bf16[8,8,2,40,512]{4,3,2,1,0:T(8,128)(2,1)} async-done(((bf16[2,8,2,40,512]{4,3,2,1,0:T(8,128)(2,1)}), bf16[8,8,2,40,512]{4,3,2,1,0:T(8,128)(2,1)}) %all-gather.25.cloned.1.call-update) | async-done | bytes 5242896 | tf_op jit(solution)/shard_map/all_gather | solution.py:48
  221.7 5.3 copy.139
  227.0 71.0 %all-gather.29.cloned.1.call-done = bf16[16,4,2,40,512]{4,3,2,1,0:T(8,128)(2,1)} async-done(((bf16[8,4,2,40,512]{4,3,2,1,0:T(8,128)(2,1)}), bf16[16,4,2,40,512]{4,3,2,1,0:T(8,128)(2,1)}) %all-gather.29.cloned.1.call-update) | async-done | bytes 5242896 | tf_op jit(solution)/shard_map/all_gather | solution.py:48
  298.0 5.3 copy.140
  303.3 72.0 %all-gather.31.cloned.1.call-done = bf16[32,2,2,48,512]{4,3,2,1,0:T(8,128)(2,1)} async-done(((bf16[4,2,2,48,512]{4,3,2,1,0:T(8,128)(2,1)}), bf16[32,2,2,48,512]{4,3,2,1,0:T(8,128)(2,1)}) %all-gather.31.cloned.1.call-update) | async-done | bytes 6291472 | tf_op jit(solution)/shard_map/all_gather | solution.py:48
  375.2 13.6 %maximum_bitcast_fusion = bf16[2,64,128,512]{3,2,0,1:T(8,128)(2,1)} fusion(bf16[64,2,48,512]{3,2,1,0:T(8,128)(2,1)} %bitcast.143, bf16[64,2,40,512]{3,2,1,0:T(8,128)(2,1)} %bitcast.135, bf16[64,2,40,512]{3,2,1,0:T(8,128)(2,1)} %bitcast.134), kind=kLoop, calls=%fused_computation.24 | loop fusion | flops 50331648 | bytes 33554432 | tf_op jit(solution)/shard_map/transpose | solution.py:17
  388.9 23.2 %copy.141 = bf16[2,64,128,512]{2,1,3,0:T(8,128)(2,1)} copy(bf16[2,64,128,512]{3,2,0,1:T(8,128)(2,1)} %maximum_bitcast_fusion) | data formatting | bytes 33554432 | tf_op jit(solution)/shard_map/transpose | solution.py:17
  412.0 25.3 %reshape.118 = bf16[2,8192,512]{1,2,0:T(8,128)(2,1)} reshape(bf16[2,64,128,512]{2,1,3,0:T(8,128)(2,1)} %copy.141) | data formatting | bytes 33554432 | tf_op jit(solution)/shard_map/reshape | solution.py:19
  437.4 31.6 %while.18 = (s32[]{:T(128)}, f32[128,4,4]{0,2,1:T(4,128)S(1)}, f32[128,4,4]{0,2,1:T(4,128)S(1)}, f32[128,4,4,128]{3,0,2,1:T(8,128)}, s32[8192]{0:T(1024)S(1)}, /...) while((s32[]{:T(128)}, f32[128,4,4]{0,2,1:T(4,128)S(1)}, ...), condition=%wide.region_11.12_spmd.clone, body=%wide.region_5.11_spmd.clone.sunk | while | flops 549196416 | bytes 27144060 | solution.py:154
  437.5 0.8 fusion.53
  439.0 5.6 conditional.3
  439.0 1.3 constant_dynamic-slice_fusion.1
  440.3 0.9 fusion.2
  441.1 0.9 fusion.6
  442.0 1.5 fusion.16
  443.6 1.0 copy-done.1
  446.3 0.8 fusion.53
  447.9 0.8 fusion.53
  449.5 0.8 fusion.53
  451.2 0.8 fusion.53
  452.8 0.8 fusion.53
  454.4 0.8 fusion.53
  456.1 0.8 fusion.53
  457.7 0.8 fusion.53
  459.3 0.8 fusion.53
  462.6 0.8 fusion.53
  469.0 2.5 copy.144
  471.5 1.3 divide_convert_fusion
  474.2 1.7 broadcast_select_fusion.1
  476.0 1.0 copy.152
  477.0 332.5 %all-reduce.3.cloned.1.call-done = (f32[4,128,512]{2,1,0:T(8,128)}, f32[4,128,512]{2,1,0:T(8,128)}) async-done(((f32[4,128,512]{2,1,0:T(8,128)}, f32[4,128,512]{2,1,0:T(8,128)}), (f32[4,128,512]{2,1,0:T(8,128)}, f32[4,128,512]{2,1,0:T(8,128)})) %all-reduce.3.cloned.1.call-update) | async-done | bytes 2097168 | tf_op jit(solution)/shard_map/psum | solution.py:188
  809.6 3.0 select_reduce_fusion
  (123 shorter events, 10.9 us)
Async XLA Ops:
  7.2 53.5 %all-gather.19.cloned.1.call-start = ((), (), s32[]{:S(2)}) async-start(), calls=%async_computation.1 | async-start | bytes 2359296 | tf_op jit(solution)/shard_map/all_gather | solution.py:36
  12.8 75.0 %all-gather.23.cloned.1.call-start = ((), (), s32[]{:S(2)}) async-start(), calls=%async_computation.3 | async-start | bytes 1966080 | tf_op jit(solution)/shard_map/all_gather | solution.py:48
  47.5 85.3 %all-gather.27.cloned.1.call-start = ((), (), s32[]{:S(2)}) async-start(), calls=%async_computation.5 | async-start | bytes 2949120 | tf_op jit(solution)/shard_map/all_gather | solution.py:48
  60.6 93.3 %copy-start.4 = (s32[1,128]{1,0:T(1,128)S(1)}, s32[1,128]{1,0:T(1,128)}, u32[]{:S(2)}) copy-start(s32[1,128]{1,0:T(1,128)} %param.15) | copy-start | bytes 1540
  60.6 102.5 %copy-start.2 = (bf16[1,128,2048]{2,1,0:T(8,128)(2,1)S(1)}, bf16[1,128,2048]{2,1,0:T(8,128)(2,1)}, u32[]{:S(2)}) copy-start(bf16[1,128,2048]{2,1,0:T(8,128)(2,1)} %param.12) | copy-start | bytes 1572868
  60.6 103.4 %all-gather.21.cloned.1.call-start = ((), (), s32[]{:S(2)}) async-start(), calls=%async_computation.2 | async-start | bytes 1310720 | tf_op jit(solution)/shard_map/all_gather | solution.py:36
  63.4 158.3 %all-gather.25.cloned.1.call-start = ((), (), s32[]{:S(2)}) async-start(), calls=%async_computation.4 | async-start | bytes 6553600 | tf_op jit(solution)/shard_map/all_gather | solution.py:48
  87.8 75.9 %copy-start.3 = (bf16[1,128,2048]{2,1,0:T(8,128)(2,1)S(1)}, bf16[1,128,2048]{2,1,0:T(8,128)(2,1)}, u32[]{:S(2)}) copy-start(bf16[1,128,2048]{2,1,0:T(8,128)(2,1)} %param.19) | copy-start | bytes 1572868
  87.8 210.1 %all-gather.29.cloned.1.call-start = ((), (), s32[]{:S(2)}) async-start(), calls=%async_computation.6 | async-start | bytes 7864320 | tf_op jit(solution)/shard_map/all_gather | solution.py:48
  132.8 242.4 %all-gather.31.cloned.1.call-start = ((), (), s32[]{:S(2)}) async-start(), calls=%async_computation.7 | async-start | bytes 7077888 | tf_op jit(solution)/shard_map/all_gather | solution.py:48
  154.5 282.8 %all-to-all-start = ((s32[64,1,128]{2,1,0:T(1,128)}), s32[64,1,128]{2,1,0:T(1,128)S(1)}, u32[]{:S(2)}, u32[]{:S(2)}) async-start(s32[64,1,128]{2,1,0:T(1,128)} %broadcast_in_dim.114), calls=%async_computation | async-start | bytes 65536 | tf_op jit(solution)/shard_map/all_to_all | solution.py:24
  163.0 646.5 %all-reduce.3.cloned.1.call-start = ((), (), s32[]{:S(2)}) async-start(), calls=%async_computation.8 | async-start | bytes 4194304 | tf_op jit(solution)/shard_map/psum | solution.py:188
  440.3 1.8 copy-start
  443.6 1.0 copy-start.1
  473.4 2.5 copy-start.5
Sparse Core Ops, SparseCore 0:
  13.0 45.0 all-gather.18
  59.8 27.9 all-gather.22
  89.6 43.1 all-gather.26
  135.0 24.7 all-gather.20
  161.5 60.1 all-gather.24
  223.3 74.6 all-gather.28
  299.8 75.3 all-gather.30
  476.1 333.4 all-reduce.2
